TPU v7x, 32 devices: a whole 2x2x4 slice. The times are simulated.
32 devices in a mesh: gx: 8 (over z, x), gy: 4 (over y, core).
Axes of the slice: x: 2, y: 2, z: 4, core: 2. Of those that a mesh axis runs over, the one named last changes fastest.
Arguments:
- velocity: float32 [3, 8192, 512], P(None, ('gx', 'gy')), may hold values from -6 to 6
- positions: float32 [3, 1024, 256], P(None, ('gx', 'gy')), may hold values from -6 to 6
- stiff_h: float32 [1024, 256], P(('gx', 'gy')), may hold values from 0.1 to 1
- stiff_v: float32 [1024, 256], P(('gx', 'gy')), may hold values from 0.1 to 1
- marker_owner: int32 [262144, 1], P(('gx', 'gy')), may hold values from 0 to 31; in each aligned block of 8192 rows (0 to 8191, 8192 to 16383, ...) at most 384 rows name the same one
- marker_element: int32 [262144], P(('gx', 'gy')), may hold values from 0 to 255
- marker_coords: float32 [3, 262144], P(None, ('gx', 'gy')), may hold values from -1 to 1
Outputs:
- new_positions: float32 [3, 1024, 256], P(None, ('gx', 'gy'))
- node_forces: float32 [3, 8192, 512], P(None, ('gx', 'gy'))
Inputs may be any that keep to these rules, and one draw needn't show every extreme that they name: `marker_owner`: among the markers of one device's rows, no owner is named more than 384 times, and in some devices' rows one owner is named exactly 384 times.
All inputs are finite; a program needn't handle non-finite values.
Results may differ from a plain program's by a relative error of at most 0.00013.
Values sent between devices are 32-bit elements; how exact they have to be, the bound alone decides.
No kernel may reach another device: no remote copies, remote signals or barrier semaphores. Data moves between devices by JAX's collectives and lax.ppermute only.
A program may use at most 64 MiB of HBM per device.

v0:
```python
import math
import jax
import jax.numpy as jnp
from jax import lax
from jax.sharding import PartitionSpec as P

POINTS = 8
bend_modulus = 0.05
time_step = 0.5


def padded(cells, sides, width):
    for axis, dim in sides:
        count = lax.axis_size(axis)
        head = lax.slice_in_dim(cells, 0, width, axis=dim)
        tail = lax.slice_in_dim(cells, cells.shape[dim] - width, cells.shape[dim], axis=dim)
        cells = jnp.concatenate(
            [
                lax.ppermute(tail, axis, [(i, (i + 1) % count) for i in range(count)]),
                cells,
                lax.ppermute(head, axis, [((i + 1) % count, i) for i in range(count)]),
            ],
            axis=dim,
        )
    return cells


def basis(values):
    abscissa = -jnp.cos(jnp.pi * jnp.arange(POINTS).astype(values.dtype) / (POINTS - 1))
    collected = []
    for i in range(POINTS):
        product = jnp.ones_like(values)
        for j in range(POINTS):
            if j != i:
                product = product * ((values - abscissa[j]) / (abscissa[i] - abscissa[j]))
        collected.append(product)
    return jnp.stack(collected)


def weight_table(factors):
    along_r = factors[0:POINTS].T
    along_s = factors[POINTS : 2 * POINTS].T
    along_t = factors[2 * POINTS : 3 * POINTS].T
    table = along_r[:, :, None, None] * along_s[:, None, :, None] * along_t[:, None, None, :]
    return table.reshape(along_r.shape[0], POINTS * POINTS * POINTS)


def surface_laplacian(extended):
    middle = extended[:, 1:-1]
    return (
        extended[:, 2:]
        + extended[:, :-2]
        + jnp.roll(middle, 1, axis=2)
        + jnp.roll(middle, -1, axis=2)
        - 4.0 * middle
    )


def tension(extended, stiff_h):
    points = extended[:3]
    vertical = extended[3]
    middle = points[:, 1:-1]
    return (
        stiff_h * (jnp.roll(middle, -1, axis=2) - middle)
        + jnp.roll(stiff_h, 1, axis=1) * (jnp.roll(middle, 1, axis=2) - middle)
        + vertical[1:-1] * (points[:, 2:] - middle)
        + vertical[:-2] * (points[:, :-2] - middle)
    )


def three_factors(coords):
    return jnp.concatenate([basis(coords[0]), basis(coords[1]), basis(coords[2])], axis=0)


def selector_of(block_elements, elem_count):
    return (block_elements[:, None] == jnp.arange(elem_count, dtype=jnp.int32)[None, :]).astype(
        jnp.float32
    )


def local(velocity, positions, stiff_h, stiff_v, marker_owner, marker_element, marker_coords):
    major_count = lax.axis_size("gx")
    minor_count = lax.axis_size("gy")
    devices_all = major_count * minor_count
    marker_count = marker_owner.shape[0]
    capacity = 3 * marker_count // (2 * devices_all)
    slot_total = devices_all * capacity
    elem_count = velocity.shape[1]
    stacked = jnp.concatenate([positions, stiff_v[None]], axis=0)
    extended = padded(stacked, ((("gx", "gy"), 1),), 1)
    pulling = tension(extended, stiff_h)
    laplace = surface_laplacian(extended[:3])
    laplace_wide = padded(laplace, ((("gx", "gy"), 1),), 1)
    bending = -bend_modulus * surface_laplacian(laplace_wide)
    marker_force = (pulling + bending).reshape(3, marker_count)
    owners = marker_owner[:, 0]
    ordering = jnp.argsort(owners, stable=True)
    sorted_owners = owners[ordering]
    offsets = jnp.searchsorted(sorted_owners, jnp.arange(devices_all, dtype=jnp.int32), side="left")
    within = jnp.arange(marker_count, dtype=jnp.int32) - offsets[sorted_owners]
    places = (
        jnp.zeros((marker_count,), jnp.int32).at[ordering].set(sorted_owners * capacity + within)
    )
    described = three_factors(marker_coords)
    lead = described.shape[0]
    payload = jnp.concatenate([described, marker_force], axis=0)
    width_all = payload.shape[0]
    outgoing = jnp.zeros((width_all, slot_total), jnp.float32).at[:, places].set(payload)
    slot_ids = jnp.zeros((1, slot_total), jnp.int32).at[:, places].set(marker_element[None])
    got_floats, got_slots = (
        lax.all_to_all(
            lax.all_to_all(
                outgoing.reshape(width_all, major_count, minor_count, capacity),
                "gx",
                split_axis=1,
                concat_axis=1,
                tiled=True,
            ),
            "gy",
            split_axis=2,
            concat_axis=2,
            tiled=True,
        ),
        lax.all_to_all(
            lax.all_to_all(
                slot_ids.reshape(1, major_count, minor_count, capacity),
                "gx",
                split_axis=1,
                concat_axis=1,
                tiled=True,
            ),
            "gy",
            split_axis=2,
            concat_axis=2,
            tiled=True,
        ),
    )
    got_floats = got_floats.reshape(width_all, slot_total)
    element_ids = got_slots.reshape(slot_total)
    factors = got_floats[:lead]
    pushes = got_floats[lead:]
    block_len = math.gcd(slot_total, 512)
    block_count = slot_total // block_len
    factor_blocks = factors.reshape(3 * POINTS, block_count, block_len).transpose(1, 0, 2)
    element_blocks = element_ids.reshape(block_count, block_len)
    push_blocks = pushes.reshape(3, block_count, block_len).transpose(1, 0, 2)

    def sample(inputs):
        block_factors, block_elements = inputs
        weights = weight_table(block_factors)
        selector = selector_of(block_elements, elem_count)
        gathered = jnp.einsum("be,ken->kbn", selector, velocity, precision=lax.Precision.HIGHEST)
        return jnp.sum(gathered * weights[None], axis=-1)

    sampled = lax.map(sample, (factor_blocks, element_blocks))
    returning = sampled.transpose(1, 0, 2).reshape(3, slot_total)
    arrived = lax.all_to_all(
        lax.all_to_all(
            returning.reshape(3, major_count, minor_count, capacity),
            "gx",
            split_axis=1,
            concat_axis=1,
            tiled=True,
        ),
        "gy",
        split_axis=2,
        concat_axis=2,
        tiled=True,
    )

    def deposit(running, inputs):
        block_factors, block_elements, block_pushes = inputs
        weights = weight_table(block_factors)
        selector = selector_of(block_elements, elem_count)
        loads = block_pushes[:, :, None] * weights[None]
        added = jnp.einsum("be,kbn->ken", selector, loads, precision=lax.Precision.HIGHEST)
        return (running + added, None)

    node_forces, unused = lax.scan(
        deposit, jnp.zeros_like(velocity), (factor_blocks, element_blocks, push_blocks)
    )
    moved = jnp.take(arrived.reshape(3, slot_total), places, axis=1).reshape(positions.shape)
    return (positions + time_step * moved, node_forces)


def solution(mesh):
    return jax.shard_map(
        local,
        mesh=mesh,
        in_specs=(
            P(None, ("gx", "gy"), None),
            P(None, ("gx", "gy"), None),
            P(("gx", "gy"), None),
            P(("gx", "gy"), None),
            P(("gx", "gy"), None),
            P(("gx", "gy")),
            P(None, ("gx", "gy")),
        ),
        out_specs=(P(None, ("gx", "gy"), None), P(None, ("gx", "gy"), None)),
        check_vma=False,
    )
```

profile of v0, /device:TPU:0, one launch (start us, length us, event | category | flops | bytes accessed | tf_op | source)
XLA Modules:
  0.0 586.4 jit_solution(10198000036078593590)
XLA Ops:
  2.0 6.0 %collective-permute-start = (f32[4,1,256]{2,1,0:T(1,128)S(1)}, f32[4,1,256]{2,1,0:T(1,128)S(1)}, u32[]{:S(2)}, u32[]{:S(2)}) collective-permute-start(f32[4,1,256]{2,1,0:T(1,128)S(1)} %get-tuple-element.267), channel_id=1, source_target_pairs={{1,0},{2,1},{3,2},{4,3},{5,4},{6,5},{7,6},{8,7},{9,8},{10,9},{11,1... | collective-permute-start | bytes 12296 | tf_op jit(solution)/shard_map/ppermute | solution.py:21
  8.0 7.5 %sort.17 = (s32[8192]{0:T(1024)}, s32[8192]{0:T(1024)S(1)}) sort(s32[8192]{0:T(1024)} %bitcast.127, s32[8192]{0:T(1024)S(1)} %iota.23), dimensions={0}, to_apply=%region_0.1 | sort | flops 106496 | bytes 131072 | tf_op jit(solution)/shard_map/jit(argsort)/sort | solution.py:97
  15.5 45.5 %gather_fusion.1 = s32[8192]{0:T(1024)S(1)} fusion(s32[8192]{0:T(1024)S(1)} %bitcast.128, s32[8192]{0:T(1024)S(1)} %get-tuple-element.305), kind=kCustom, calls=%fused_computation.1 | custom fusion | bytes 98304 | tf_op jit(solution)/shard_map/gather | solution.py:98
  61.1 10.5 %while.46 = (s32[]{:T(128)}, u32[32]{0:T(128)S(1)}, u32[32]{0:T(128)S(1)}, s32[8192]{0:T(1024)S(1)}, s32[]{:T(128)}, /*index=5*/s32[]{:T(128)}, s32[]{}) while((s32[]{:T(128)}, u32[32]{0:T(128)S(1)}, u32[32]{0:T(128)S(1)}, s32[8192]{0:T(1024)S(1)}, s32[]{:T(128)}, /*index=5*/s32[]{:T(128)}, s32[]{}) %tuple.172), condition=%wide.region_2.3_spmd.clone, body=%wide.region_1.2_spmd.clone.sunk | while | flops 1444 | bytes 5732 | solution.py:99
  80.0 15.9 %fusion.35 = s32[8192]{0:T(1024)S(1)} fusion(pred[8192]{0:T(1024)(128)(4,1)S(1)} %get-tuple-element.228, pred[8192]{0:T(1024)(128)(4,1)S(1)} %get-tuple-element.227, pred[8192]{0:T(1024)(128)(4,1)S(1)} %get-tuple-element.226, pred[8192]{0:T(1024)(128)(4,1)S(1)} %get-tuple-element.225, pred[8192]{0:T(1024)(128)(4,1)S(1)} %get-tuple-element.224, ...), kind=kLoop, calls=%fused_computation.250 | loop fusion | flops 229376 | bytes 303204 | tf_op jit(solution)/shard_map/add | solution.py:102
  95.9 30.5 %scatter_custom_fusion = s32[8192]{0:T(1024)S(1)} fusion(s32[8192]{0:T(1024)S(1)} %get-tuple-element.306, s32[8192]{0:T(1024)S(1)} %fusion.35, s32[]{:T(128)} %constant.79.clone.1), kind=kCustom, calls=%fused_computation.280 | custom fusion | bytes 32772 | tf_op jit(solution)/shard_map/scatter | solution.py:102
  126.4 30.7 %scatter_custom_fusion.1 = s32[12288]{0:T(1024)S(1)} fusion(s32[8192]{0:T(1024)S(1)} %get-tuple-element.304, s32[8192]{0:T(1024)} %param.18, s32[]{:T(128)} %constant.79.clone.1), kind=kCustom, calls=%fused_computation.252 | custom fusion | bytes 49664 | tf_op jit(solution)/shard_map/scatter | solution.py:109
  231.5 4.8 divide_multiply_fusion
  236.3 4.9 divide_multiply_fusion.6
  241.2 4.9 divide_multiply_fusion.12
  246.1 4.9 divide_multiply_fusion.18
  250.9 4.9 divide_multiply_fusion.24
  255.8 4.9 divide_multiply_fusion.30
  260.7 4.8 divide_multiply_fusion.36
  265.5 4.9 divide_multiply_fusion.42
  274.9 5.3 collective-permute-done.3
  284.4 23.9 %scatter_custom_fusion.2 = f32[27,12288]{0,1:T(8,128)} fusion(s32[8192]{0:T(1024)S(1)} %get-tuple-element.304, f32[8192,27]{1,0:T(8,128)} %copy.89, f32[]{:T(128)} %constant.87.clone.1), kind=kCustom, calls=%fused_computation.41 | custom fusion | bytes 1327616 | tf_op jit(solution)/shard_map/scatter | solution.py:108
  308.2 5.5 copy.90
  318.0 26.6 %all-to-all-done.2 = f32[27,8,4,384]{3,2,0,1:T(4,128)S(1)} async-done(((f32[27,8,4,384]{3,2,0,1:T(4,128)}), f32[27,8,4,384]{3,2,0,1:T(4,128)S(1)}, u32[]{:S(2)}, u32[]{:S(2)}) %all-to-all-start.2) | async-done | bytes 1327136 | tf_op jit(solution)/shard_map/all_to_all | solution.py:112
  357.5 16.7 %all-to-all-done.3 = f32[27,8,4,384]{3,1,0,2:T(8,128)} async-done(((f32[27,8,4,384]{3,1,0,2:T(8,128)}), f32[27,8,4,384]{3,1,0,2:T(8,128)}, u32[]{:S(2)}, u32[]{:S(2)}) %all-to-all-start.3) | async-done | bytes 1327136 | tf_op jit(solution)/shard_map/all_to_all | solution.py:111
  380.9 64.9 %while.45 = (s32[]{:T(128)}, f32[24,3,512]{2,1,0:T(4,128)S(1)}, s32[24,512]{1,0:T(8,128)S(1)}, f32[3,256,512]{1,2,0:T(8,128)S(1)}, f32[24,24,512]{2,1,0:T(8,128)}, /*index=5*/s32[]{:T(128)}, s32[]{:T(128)}, s32[]{}, s32[]{}) while((s32[]{:T(128)}, f32[24,3,512]{2,1,0:T(4,128)S(1)}, s32[24,512]{1,0:T(8,128)S(1)}, f32[3,256,512]{1,2,0:T(8,128)S(1)}, ...), condition=%wide.region_8.9_spmd, body=%wide.region_6.8_spmd.sunk | while | flops 2417916416 | bytes 4108425 | solution.py:155
  451.5 6.4 %all-to-all-done.4 = f32[3,8,4,384]{3,2,0,1:T(4,128)S(1)} async-done(((f32[3,8,4,384]{3,2,0,1:T(4,128)}), f32[3,8,4,384]{3,2,0,1:T(4,128)S(1)}, u32[]{:S(2)}, u32[]{:S(2)}) %all-to-all-start.4) | async-done | bytes 147488 | tf_op jit(solution)/shard_map/all_to_all | solution.py:158
  461.8 85.0 %while.47 = (s32[]{:T(128)}, f32[3,256,512]{1,2,0:T(8,128)S(1)}, f32[24,3,512]{2,0,1:T(8,128)S(1)}, f32[24,24,512]{2,1,0:T(8,128)}, s32[24,512]{1,0:T(8,128)S(1)}, /*index=5*/s32[]{:T(128)}, s32[]{:T(128)}, s32[]{}, s32[]{}) while((s32[]{:T(128)}, f32[3,256,512]{1,2,0:T(8,128)S(1)}, f32[24,3,512]{2,0,1:T(8,128)S(1)}, ...), condition=%wide.region_10.11_spmd.clone, body=%wide.region_9.10_spmd.clone.sunk | while | flops 2417917952 | bytes 5689491 | solution.py:179
  552.4 30.5 %gather_fusion.2 = f32[8192,3]{1,0:T(8,128)} fusion(f32[3,12288]{0,1:T(8,128)} %bitcast.133, s32[8192]{0:T(1024)S(1)} %get-tuple-element.303), kind=kCustom, calls=%fused_computation.2 | custom fusion | bytes 229376 | tf_op jit(solution)/shard_map/jit(_take)/gather | solution.py:182
  (446 shorter events, 223.5 us)
Async XLA Ops:
  0.6 14.9 %copy-start = (s32[8192,1]{0,1:T(1,128)S(1)}, s32[8192,1]{0,1:T(1,128)}, u32[]{:S(2)}) copy-start(s32[8192,1]{0,1:T(1,128)} %param.17) | copy-start | bytes 98308
  1.4 269.1 %collective-permute-start.1 = (f32[4,1,256]{2,1,0:T(1,128)S(1)}, f32[4,1,256]{2,1,0:T(1,128)S(1)}, u32[]{:S(2)}, u32[]{:S(2)}) collective-permute-start(f32[4,1,256]{2,1,0:T(1,128)S(1)} %get-tuple-element.268), channel_id=1, source_target_pairs={{0,1},{1,2},{2,3},{3,4},{4,5},{5,6},{6,7},{7,8},{8,9},{9,10},{10,1... | collective-permute-start | bytes 12296 | tf_op jit(solution)/shard_map/ppermute | solution.py:19
  2.0 268.6 %collective-permute-start = (f32[4,1,256]{2,1,0:T(1,128)S(1)}, f32[4,1,256]{2,1,0:T(1,128)S(1)}, u32[]{:S(2)}, u32[]{:S(2)}) collective-permute-start(f32[4,1,256]{2,1,0:T(1,128)S(1)} %get-tuple-element.267), channel_id=1, source_target_pairs={{1,0},{2,1},{3,2},{4,3},{5,4},{6,5},{7,6},{8,7},{9,8},{10,9},{11,1... | collective-permute-start | bytes 12296 | tf_op jit(solution)/shard_map/ppermute | solution.py:21
  61.0 170.1 %copy-start.1 = (f32[3,32,256]{2,1,0:T(8,128)S(1)}, f32[3,32,256]{2,1,0:T(8,128)}, u32[]{:S(2)}) copy-start(f32[3,32,256]{2,1,0:T(8,128)} %param.14) | copy-start | bytes 294916
  71.6 159.8 %copy-start.5 = (f32[32,256]{1,0:T(8,128)S(1)}, f32[32,256]{1,0:T(8,128)}, u32[]{:S(2)}) copy-start(f32[32,256]{1,0:T(8,128)} %param.15) | copy-start | bytes 98308
  71.6 159.8 %copy-start.2 = (f32[3,8192]{1,0:T(4,128)S(1)}, f32[3,8192]{1,0:T(4,128)}, u32[]{:S(2)}) copy-start(f32[3,8192]{1,0:T(4,128)} %param.19) | copy-start | bytes 294916
  80.0 190.5 %copy-start.4 = (f32[32,256]{1,0:T(8,128)S(1)}, f32[32,256]{1,0:T(8,128)}, u32[]{:S(2)}) copy-start(f32[32,256]{1,0:T(8,128)} %param.16) | copy-start | bytes 98308
  157.8 156.0 %all-to-all-start = ((s32[1,8,4,384]{3,2,0,1:T(4,128)}), s32[1,8,4,384]{3,2,0,1:T(4,128)S(1)}, u32[]{:S(2)}, u32[]{:S(2)}) async-start(s32[1,8,4,384]{3,2,0,1:T(4,128)} %reshape.123), calls=%async_computation | async-start | bytes 98304 | tf_op jit(solution)/shard_map/all_to_all | solution.py:125
  270.9 4.0 collective-permute-start.2
  273.5 6.6 %collective-permute-start.3 = (f32[3,1,256]{2,1,0:T(1,128)S(1)}, f32[3,1,256]{2,1,0:T(1,128)S(1)}, u32[]{:S(2)}, u32[]{:S(2)}) collective-permute-start(f32[3,1,256]{2,1,0:T(1,128)S(1)} %get-tuple-element.298), channel_id=1, source_target_pairs={{0,1},{1,2},{2,3},{3,4},{4,5},{5,6},{6,7},{7,8},{8,9},{9,10},{10,1... | collective-permute-start | bytes 9224 | tf_op jit(solution)/shard_map/ppermute | solution.py:19
  313.8 30.8 %all-to-all-start.2 = ((f32[27,8,4,384]{3,2,0,1:T(4,128)}), f32[27,8,4,384]{3,2,0,1:T(4,128)S(1)}, u32[]{:S(2)}, u32[]{:S(2)}) async-start(f32[27,8,4,384]{3,2,0,1:T(4,128)} %copy.90), calls=%async_computation.2 | async-start | bytes 2654208 | tf_op jit(solution)/shard_map/all_to_all | solution.py:112
  344.6 7.8 %all-to-all-start.1 = ((s32[1,8,4,384]{3,1,0,2:T(8,128)}), s32[1,8,4,384]{3,1,0,2:T(8,128)S(1)}, u32[]{:S(2)}, u32[]{:S(2)}) async-start(s32[1,8,4,384]{3,1,0,2:T(8,128)} %copy.87), calls=%async_computation.1 | async-start | bytes 98304 | tf_op jit(solution)/shard_map/all_to_all | solution.py:124
  349.5 7.4 %copy-start.3 = (f32[3,256,512]{2,1,0:T(8,128)S(1)}, f32[3,256,512]{2,1,0:T(8,128)}, u32[]{:S(2)}) copy-start(f32[3,256,512]{2,1,0:T(8,128)} %param.13) | copy-start | bytes 4718596
  352.4 21.8 %all-to-all-start.3 = ((f32[27,8,4,384]{3,1,0,2:T(8,128)}), f32[27,8,4,384]{3,1,0,2:T(8,128)}, u32[]{:S(2)}, u32[]{:S(2)}) async-start(f32[27,8,4,384]{3,1,0,2:T(8,128)} %copy.91), calls=%async_computation.3 | async-start | bytes 2654208 | tf_op jit(solution)/shard_map/all_to_all | solution.py:111
  446.6 11.2 %all-to-all-start.4 = ((f32[3,8,4,384]{3,2,0,1:T(4,128)}), f32[3,8,4,384]{3,2,0,1:T(4,128)S(1)}, u32[]{:S(2)}, u32[]{:S(2)}) async-start(f32[3,8,4,384]{3,2,0,1:T(4,128)} %copy.96), calls=%async_computation.4 | async-start | bytes 294912 | tf_op jit(solution)/shard_map/all_to_all | solution.py:158
  458.5 90.0 %all-to-all-start.5 = ((f32[3,8,4,384]{3,1,0,2:T(8,128)}), f32[3,8,4,384]{3,1,0,2:T(8,128)S(1)}, u32[]{:S(2)}, u32[]{:S(2)}) async-start(f32[3,8,4,384]{3,1,0,2:T(8,128)} %copy.97), calls=%async_computation.5 | async-start | bytes 294912 | tf_op jit(solution)/shard_map/all_to_all | solution.py:157
where the time goes:
time: 596 us; the launch traced here: 586 us
  local copies, waits for them, and re-layouts  242 us (41%)
  matrix products  103 us (17%)
  other arithmetic  78.1 us (13%)
  between operations  70.2 us (12%)
  waiting for transfers between devices  59.2 us (10%)
  starting transfers between devices  31.7 us (5%)
    dot_general x24, matrix products, deposit(): jnp.einsum('be,kbn->ken', selector, loads, precision=lax.Precision.HIGHEST)  60.9 us
    gather x1, local copies, waits for them, and re-layouts, local(): sorted_owners = owners[ordering]  45.5 us
    dot_general x24, matrix products, sample(): jnp.einsum('be,ken->kbn', selector, velocity, precision=lax.Precision.HIG...  41.8 us
    mul x8, other arithmetic, basis(): product = product * ((values - abscissa[j]) / (abscissa[i] - abscissa[j]))  39 us
    transpose x48, local copies, waits for them, and re-layouts, weight_table(): along_r = factors[0:POINTS].T  36.7 us
    gather x2, local copies, waits for them, and re-layouts, local(): jnp.take(arrived.reshape(3, slot_total), places, axis=1)  33.3 us
    scatter x1, local copies, waits for them, and re-layouts, local(): jnp.zeros((1, slot_total), jnp.int32).at[:, places]  30.7 us
    scatter x1, local copies, waits for them, and re-layouts, local(): jnp.zeros((marker_count,), jnp.int32).at[ordering]  30.5 us
  transfers between devices with their start and end apart: 10, of which 6 were waited for; matrix products, arithmetic and copies ran while one was open for 53% of the time, Pallas kernels for 0%

commit v1 on v0

--- a/solution.py
+++ b/solution.py
@@ -7,6 +7,30 @@
 POINTS = 8
 bend_modulus = 0.05
 time_step = 0.5
+
+
+def split_up(x, dim, size):
+    shape = x.shape
+    blocks = x.reshape(*shape[:dim], size, shape[dim] // size, *shape[dim + 1 :])
+    return jnp.moveaxis(blocks, dim, 0)
+
+
+def laid_out(parts, dim):
+    shape = list(parts.shape[1:])
+    shape[dim] *= parts.shape[0]
+    return jnp.moveaxis(parts, 0, dim).reshape(shape)
+
+
+def rotated_exchange(value, axis, split_dim, concat_dim):
+    size, index = (lax.axis_size(axis), lax.axis_index(axis))
+    parts = split_up(value, split_dim, size)
+    result = parts
+    for step in range(1, size):
+        target, source = ((index + step) % size, (index - step) % size)
+        sent = lax.dynamic_index_in_dim(parts, target, 0)
+        theirs = lax.ppermute(sent, axis, [(i, (i + step) % size) for i in range(size)])
+        result = lax.dynamic_update_slice_in_dim(result, theirs, source, axis=0)
+    return laid_out(result, concat_dim)
 
 
 def padded(cells, sides, width):
@@ -108,7 +132,7 @@
     outgoing = jnp.zeros((width_all, slot_total), jnp.float32).at[:, places].set(payload)
     slot_ids = jnp.zeros((1, slot_total), jnp.int32).at[:, places].set(marker_element[None])
     got_floats, got_slots = (
-        lax.all_to_all(
+        rotated_exchange(
             lax.all_to_all(
                 outgoing.reshape(width_all, major_count, minor_count, capacity),
                 "gx",
@@ -117,9 +141,8 @@
                 tiled=True,
             ),
             "gy",
-            split_axis=2,
-            concat_axis=2,
-            tiled=True,
+            2,
+            2,
         ),
         lax.all_to_all(
             lax.all_to_all(

time: 596 us -> 623 us (1.045)
  local copies, waits for them, and re-layouts: 242 us -> 280 us
  waiting for transfers between devices: 59.2 us -> 42.7 us
  blocking collectives: 0 us -> 10.8 us
  starting transfers between devices: 31.7 us -> 24.2 us
    dynamic_update_slice x0 -> x3, local copies, waits for them, and re-layouts: none -> 35.9 us  [rotated_exchange(): result = lax.dynamic_update_slice_in_dim(result, theirs, source, axis=0)]
    all_to_all x2 -> x0, waiting for transfers between devices: 16.7 us -> none  [the longest x1 16.7 us: local(): lax.all_to_all(lax.all_to_all(outgoing.reshape(width_all, major_count, mi...]
    all_to_all x0 -> x1, blocking collectives: none -> 10.8 us  [local(): lax.all_to_all(slot_ids.reshape(1, major_count, minor_count, capacity), '...]
    all_to_all x2 -> x0, starting transfers between devices: 8.03 us -> none  [the longest x1 4.5 us: local(): lax.all_to_all(lax.all_to_all(outgoing.reshape(width_all, major_count, mi...]
  transfers between devices with their start and end apart: 10 -> 11, of which waited for: 6 -> 5; matrix products, arithmetic and copies ran while one was open for 53% -> 49% of each run, Pallas kernels for 0% -> 0%
where the time goes in v1:
time: 623 us; the launch traced here: 613 us
  local copies, waits for them, and re-layouts  280 us (45%)
  matrix products  103 us (17%)
  other arithmetic  78.4 us (13%)
  between operations  71 us (11%)
  waiting for transfers between devices  42.7 us (7%)
  starting transfers between devices  24.2 us (4%)
  blocking collectives  10.8 us (2%)
    dot_general x24, matrix products, deposit(): jnp.einsum('be,kbn->ken', selector, loads, precision=lax.Precision.HIGHEST)  60.9 us
    gather x1, local copies, waits for them, and re-layouts, local(): sorted_owners = owners[ordering]  45.5 us
    dot_general x24, matrix products, sample(): jnp.einsum('be,ken->kbn', selector, velocity, precision=lax.Precision.HIG...  41.8 us
    mul x8, other arithmetic, basis(): product = product * ((values - abscissa[j]) / (abscissa[i] - abscissa[j]))  39.2 us
    transpose x48, local copies, waits for them, and re-layouts, weight_table(): along_r = factors[0:POINTS].T  36.7 us
    dynamic_update_slice x3, local copies, waits for them, and re-layouts, rotated_exchange(): result = lax.dynamic_update_slice_in_dim(result, theirs, source, axis=0)  35.9 us
    gather x2, local copies, waits for them, and re-layouts, local(): jnp.take(arrived.reshape(3, slot_total), places, axis=1)  33.3 us
    scatter x1, local copies, waits for them, and re-layouts, local(): jnp.zeros((1, slot_total), jnp.int32).at[:, places]  30.7 us
  transfers between devices with their start and end apart: 11, of which 5 were waited for; matrix products, arithmetic and copies ran while one was open for 49% of the time, Pallas kernels for 0%

profile of v1, /device:TPU:0, one launch (start us, length us, event | category | flops | bytes accessed | tf_op | source)
XLA Modules:
  0.0 613.0 jit_solution(13244898614364596956)
XLA Ops:
  2.0 6.0 collective-permute-start
  80.4 7.5 %sort.17 = (s32[8192]{0:T(1024)}, s32[8192]{0:T(1024)S(1)}) sort(s32[8192]{0:T(1024)} %bitcast.141, s32[8192]{0:T(1024)S(1)} %iota.23), dimensions={0}, to_apply=%region_0.1 | sort | flops 106496 | bytes 131072 | tf_op jit(solution)/shard_map/jit(argsort)/sort | solution.py:121
  88.0 45.5 %gather_fusion.1 = s32[8192]{0:T(1024)S(1)} fusion(s32[8192]{0:T(1024)S(1)} %bitcast.142, s32[8192]{0:T(1024)S(1)} %get-tuple-element.308), kind=kCustom, calls=%fused_computation.1 | custom fusion | bytes 98304 | tf_op jit(solution)/shard_map/gather | solution.py:122
  133.6 10.5 %while.46 = (s32[]{:T(128)}, u32[32]{0:T(128)S(1)}, u32[32]{0:T(128)S(1)}, s32[8192]{0:T(1024)S(1)}, s32[]{:T(128)}, /*index=5*/s32[]{:T(128)}, s32[]{}) while((s32[]{:T(128)}, u32[32]{0:T(128)S(1)}, u32[32]{0:T(128)S(1)}, s32[8192]{0:T(1024)S(1)}, s32[]{:T(128)}, /*index=5*/s32[]{:T(128)}, s32[]{}) %tuple.174), condition=%wide.region_2.3_spmd.clone, body=%wide.region_1.2_spmd.clone.sunk | while | flops 1444 | bytes 5732 | solution.py:123
  152.6 15.9 %fusion.35 = s32[8192]{0:T(1024)S(1)} fusion(pred[8192]{0:T(1024)(128)(4,1)S(1)} %get-tuple-element.228, pred[8192]{0:T(1024)(128)(4,1)S(1)} %get-tuple-element.227, pred[8192]{0:T(1024)(128)(4,1)S(1)} %get-tuple-element.226, pred[8192]{0:T(1024)(128)(4,1)S(1)} %get-tuple-element.225, pred[8192]{0:T(1024)(128)(4,1)S(1)} %get-tuple-element.224, ...), kind=kLoop, calls=%fused_computation.253 | loop fusion | flops 229376 | bytes 303204 | tf_op jit(solution)/shard_map/add | solution.py:126
  168.5 30.7 %scatter_custom_fusion = s32[8192]{0:T(1024)S(1)} fusion(s32[8192]{0:T(1024)S(1)} %get-tuple-element.309, s32[8192]{0:T(1024)S(1)} %fusion.35, s32[]{:T(128)} %constant.126.clone.1), kind=kCustom, calls=%fused_computation.283 | custom fusion | bytes 32772 | tf_op jit(solution)/shard_map/scatter | solution.py:126
  199.2 5.0 divide_multiply_fusion
  209.0 4.9 divide_multiply_fusion.12
  213.9 4.9 divide_multiply_fusion.18
  218.9 4.9 divide_multiply_fusion.24
  223.8 5.0 divide_multiply_fusion.30
  240.9 5.3 collective-permute-done.3
  250.4 23.9 %scatter_custom_fusion.2 = f32[27,12288]{0,1:T(8,128)} fusion(s32[8192]{0:T(1024)S(1)} %get-tuple-element.307, f32[8192,27]{1,0:T(8,128)} %copy.88, f32[]{:T(128)} %constant.134.clone.1), kind=kCustom, calls=%fused_computation.41 | custom fusion | bytes 1327616 | tf_op jit(solution)/shard_map/scatter | solution.py:132
  274.3 5.5 copy.89
  283.4 26.8 %all-to-all-done.2 = f32[27,8,4,384]{3,2,0,1:T(4,128)S(1)} async-done(((f32[27,8,4,384]{3,2,0,1:T(4,128)}), f32[27,8,4,384]{3,2,0,1:T(4,128)S(1)}, u32[]{:S(2)}, u32[]{:S(2)}) %all-to-all-start.2) | async-done | bytes 1327136 | tf_op jit(solution)/shard_map/all_to_all | solution.py:136
  315.4 30.7 %scatter_custom_fusion.1 = s32[12288]{0:T(1024)S(1)} fusion(s32[8192]{0:T(1024)S(1)} %get-tuple-element.307, s32[8192]{0:T(1024)} %param.18, s32[]{:T(128)} %constant.126.clone.1), kind=kCustom, calls=%fused_computation.255 | custom fusion | bytes 49664 | tf_op jit(solution)/shard_map/scatter | solution.py:133
  346.1 10.8 %all_to_all.25 = s32[1,8,4,384]{3,2,0,1:T(4,128)S(1)} all-to-all(s32[1,8,4,384]{3,2,0,1:T(4,128)S(1)} %reshape.134), channel_id=1, replica_groups=mesh['gx'=8,'gy'=4] {'gx'}, dimensions={1} | all-to-all | bytes 98304 | tf_op jit(solution)/shard_map/all_to_all | solution.py:148
  364.8 12.0 %dynamic_update_slice.13 = f32[4,27,8,1,384]{4,0,1,2,3:T(4,128)S(1)} dynamic-update-slice(f32[4,27,8,1,384]{4,0,1,2,3:T(4,128)S(1)} %bitcast.147, f32[1,27,8,1,384]{4,0,1,2,3:T(1,128)} %collective-permute-done.4, s32[]{:T(128)S(6)} %select_n.90, s32[]{:T(128)} %constant.126.clone.1, s32[]{:T(128)} %constant.126.clone.1, s32[]{:T(128)} %constant.126.clone.1, s32[]{:T(128)} %constant.126.clone.1) | dynamic-update-slice | bytes 663556 | tf_op jit(solution)/shard_map/dynamic_update_slice | solution.py:32
  376.8 12.0 %dynamic_update_slice.14 = f32[4,27,8,1,384]{4,0,1,2,3:T(4,128)S(1)} dynamic-update-slice(f32[4,27,8,1,384]{4,0,1,2,3:T(4,128)S(1)} %dynamic_update_slice.13, f32[1,27,8,1,384]{4,0,1,2,3:T(1,128)} %collective-permute-done.5, s32[]{:T(128)S(6)} %select_n.94, s32[]{:T(128)} %constant.126.clone.1, s32[]{:T(128)} %constant.126.clone.1, s32[]{:T(128)} %constant.126.clone.1, s32[]{:T(128)} %constant.126.clone.1) | dynamic-update-slice | bytes 663556 | tf_op jit(solution)/shard_map/dynamic_update_slice | solution.py:32
  388.7 12.0 %dynamic_update_slice.15 = f32[4,27,8,1,384]{4,0,1,2,3:T(4,128)S(1)} dynamic-update-slice(f32[4,27,8,1,384]{4,0,1,2,3:T(4,128)S(1)} %dynamic_update_slice.14, f32[1,27,8,1,384]{4,0,1,2,3:T(1,128)} %collective-permute-done.6, s32[]{:T(128)S(6)} %select_n.98, s32[]{:T(128)} %constant.126.clone.1, s32[]{:T(128)} %constant.126.clone.1, s32[]{:T(128)} %constant.126.clone.1, s32[]{:T(128)} %constant.126.clone.1) | dynamic-update-slice | bytes 663556 | tf_op jit(solution)/shard_map/dynamic_update_slice | solution.py:32
  408.1 64.9 %while.45 = (s32[]{:T(128)}, f32[24,3,512]{2,1,0:T(4,128)S(1)}, s32[24,512]{1,0:T(8,128)S(1)}, f32[3,256,512]{1,2,0:T(8,128)S(1)}, f32[24,24,512]{2,1,0:T(8,128)}, /*index=5*/s32[]{:T(128)}, s32[]{:T(128)}, s32[]{}, s32[]{}) while((s32[]{:T(128)}, f32[24,3,512]{2,1,0:T(4,128)S(1)}, s32[24,512]{1,0:T(8,128)S(1)}, f32[3,256,512]{1,2,0:T(8,128)S(1)}, ...), condition=%wide.region_8.9_spmd, body=%wide.region_6.8_spmd.sunk | while | flops 2417916416 | bytes 4108425 | solution.py:178
  477.3 7.2 %all-to-all-done.3 = f32[3,8,4,384]{3,2,0,1:T(4,128)S(1)} async-done(((f32[3,8,4,384]{3,2,0,1:T(4,128)}), f32[3,8,4,384]{3,2,0,1:T(4,128)S(1)}, u32[]{:S(2)}, u32[]{:S(2)}) %all-to-all-start.3) | async-done | bytes 147488 | tf_op jit(solution)/shard_map/all_to_all | solution.py:181
  488.5 84.9 %while.47 = (s32[]{:T(128)}, f32[3,256,512]{1,2,0:T(8,128)S(1)}, f32[24,3,512]{2,0,1:T(8,128)S(1)}, f32[24,24,512]{2,1,0:T(8,128)}, s32[24,512]{1,0:T(8,128)S(1)}, /*index=5*/s32[]{:T(128)}, s32[]{:T(128)}, s32[]{}, s32[]{}) while((s32[]{:T(128)}, f32[3,256,512]{1,2,0:T(8,128)S(1)}, f32[24,3,512]{2,0,1:T(8,128)S(1)}, ...), condition=%wide.region_10.11_spmd.clone, body=%wide.region_9.10_spmd.clone.sunk | while | flops 2417917952 | bytes 5689491 | solution.py:202
  579.0 30.5 %gather_fusion.2 = f32[8192,3]{1,0:T(8,128)} fusion(f32[3,12288]{0,1:T(8,128)} %bitcast.150, s32[8192]{0:T(1024)S(1)} %get-tuple-element.306), kind=kCustom, calls=%fused_computation.2 | custom fusion | bytes 229376 | tf_op jit(solution)/shard_map/jit(_take)/gather | solution.py:205
  (452 shorter events, 232.5 us)
Async XLA Ops:
  0.6 87.4 %copy-start = (s32[8192,1]{0,1:T(1,128)S(1)}, s32[8192,1]{0,1:T(1,128)}, u32[]{:S(2)}) copy-start(s32[8192,1]{0,1:T(1,128)} %param.17) | copy-start | bytes 98308
  1.4 237.1 %collective-permute-start.1 = (f32[4,1,256]{2,1,0:T(1,128)S(1)}, f32[4,1,256]{2,1,0:T(1,128)S(1)}, u32[]{:S(2)}, u32[]{:S(2)}) collective-permute-start(f32[4,1,256]{2,1,0:T(1,128)S(1)} %get-tuple-element.271), channel_id=1, source_target_pairs={{0,1},{1,2},{2,3},{3,4},{4,5},{5,6},{6,7},{7,8},{8,9},{9,10},{10,1... | collective-permute-start | bytes 12296 | tf_op jit(solution)/shard_map/ppermute | solution.py:43
  2.0 236.5 %collective-permute-start = (f32[4,1,256]{2,1,0:T(1,128)S(1)}, f32[4,1,256]{2,1,0:T(1,128)S(1)}, u32[]{:S(2)}, u32[]{:S(2)}) collective-permute-start(f32[4,1,256]{2,1,0:T(1,128)S(1)} %get-tuple-element.270), channel_id=1, source_target_pairs={{1,0},{2,1},{3,2},{4,3},{5,4},{6,5},{7,6},{8,7},{9,8},{10,9},{11,1... | collective-permute-start | bytes 12296 | tf_op jit(solution)/shard_map/ppermute | solution.py:45
  133.5 12.0 %copy-start.4 = (f32[32,256]{1,0:T(8,128)S(1)}, f32[32,256]{1,0:T(8,128)}, u32[]{:S(2)}) copy-start(f32[32,256]{1,0:T(8,128)} %param.15) | copy-start | bytes 98308
  133.5 65.6 %copy-start.2 = (f32[3,8192]{1,0:T(4,128)S(1)}, f32[3,8192]{1,0:T(4,128)}, u32[]{:S(2)}) copy-start(f32[3,8192]{1,0:T(4,128)} %param.19) | copy-start | bytes 294916
  144.1 94.4 %copy-start.1 = (f32[3,32,256]{2,1,0:T(8,128)S(1)}, f32[3,32,256]{2,1,0:T(8,128)}, u32[]{:S(2)}) copy-start(f32[3,32,256]{2,1,0:T(8,128)} %param.14) | copy-start | bytes 294916
  144.1 94.4 %copy-start.3 = (f32[32,256]{1,0:T(8,128)S(1)}, f32[32,256]{1,0:T(8,128)}, u32[]{:S(2)}) copy-start(f32[32,256]{1,0:T(8,128)} %param.16) | copy-start | bytes 98308
  238.8 2.0 collective-permute-start.2
  239.6 6.6 %collective-permute-start.3 = (f32[3,1,256]{2,1,0:T(1,128)S(1)}, f32[3,1,256]{2,1,0:T(1,128)S(1)}, u32[]{:S(2)}, u32[]{:S(2)}) collective-permute-start(f32[3,1,256]{2,1,0:T(1,128)S(1)} %get-tuple-element.301), channel_id=1, source_target_pairs={{0,1},{1,2},{2,3},{3,4},{4,5},{5,6},{6,7},{7,8},{8,9},{9,10},{10,1... | collective-permute-start | bytes 9224 | tf_op jit(solution)/shard_map/ppermute | solution.py:43
  279.8 30.4 %all-to-all-start.2 = ((f32[27,8,4,384]{3,2,0,1:T(4,128)}), f32[27,8,4,384]{3,2,0,1:T(4,128)S(1)}, u32[]{:S(2)}, u32[]{:S(2)}) async-start(f32[27,8,4,384]{3,2,0,1:T(4,128)} %copy.89), calls=%async_computation.2 | async-start | bytes 2654208 | tf_op jit(solution)/shard_map/all_to_all | solution.py:136
  311.9 52.8 %collective-permute-start.4 = (f32[1,27,8,1,384]{4,0,1,2,3:T(1,128)}, f32[1,27,8,1,384]{4,0,1,2,3:T(1,128)}, u32[]{:S(2)}, u32[]{:S(2)}) collective-permute-start(f32[1,27,8,1,384]{4,0,1,2,3:T(1,128)} %get-tuple-element.269), channel_id=1, source_target_pairs={{0,1},{1,2},{2,3},{3,0},{4,5},{5,6},{6,7},{7,4},{8,9},{9,10},{10,1... | collective-permute-start | bytes 995336 | tf_op jit(solution)/shard_map/ppermute | solution.py:31
  311.9 64.8 %collective-permute-start.5 = (f32[1,27,8,1,384]{4,0,1,2,3:T(1,128)}, f32[1,27,8,1,384]{4,0,1,2,3:T(1,128)}, u32[]{:S(2)}, u32[]{:S(2)}) collective-permute-start(f32[1,27,8,1,384]{4,0,1,2,3:T(1,128)} %get-tuple-element.268), channel_id=1, source_target_pairs={{0,2},{1,3},{2,0},{3,1},{4,6},{5,7},{6,4},{7,5},{8,10},{9,11},{10,... | collective-permute-start | bytes 995336 | tf_op jit(solution)/shard_map/ppermute | solution.py:31
  314.8 73.9 %collective-permute-start.6 = (f32[1,27,8,1,384]{4,0,1,2,3:T(1,128)S(1)}, f32[1,27,8,1,384]{4,0,1,2,3:T(1,128)}, u32[]{:S(2)}, u32[]{:S(2)}) collective-permute-start(f32[1,27,8,1,384]{4,0,1,2,3:T(1,128)S(1)} %get-tuple-element.267), channel_id=1, source_target_pairs={{0,3},{1,0},{2,1},{3,2},{4,7},{5,4},{6,5},{7,6},{8,11},{9,8},{10,9... | collective-permute-start | bytes 995336 | tf_op jit(solution)/shard_map/ppermute | solution.py:31
  357.4 7.3 %all-to-all-start.1 = ((s32[1,8,4,384]{3,1,0,2:T(8,128)}), s32[1,8,4,384]{3,1,0,2:T(8,128)S(1)}, u32[]{:S(2)}, u32[]{:S(2)}) async-start(s32[1,8,4,384]{3,1,0,2:T(8,128)} %copy.86), calls=%async_computation.1 | async-start | bytes 98304 | tf_op jit(solution)/shard_map/all_to_all | solution.py:147
  405.1 3.0 copy-start.5
  473.7 10.8 %all-to-all-start.3 = ((f32[3,8,4,384]{3,2,0,1:T(4,128)}), f32[3,8,4,384]{3,2,0,1:T(4,128)S(1)}, u32[]{:S(2)}, u32[]{:S(2)}) async-start(f32[3,8,4,384]{3,2,0,1:T(4,128)} %copy.94), calls=%async_computation.3 | async-start | bytes 294912 | tf_op jit(solution)/shard_map/all_to_all | solution.py:181
  485.2 89.9 %all-to-all-start.4 = ((f32[3,8,4,384]{3,1,0,2:T(8,128)}), f32[3,8,4,384]{3,1,0,2:T(8,128)S(1)}, u32[]{:S(2)}, u32[]{:S(2)}) async-start(f32[3,8,4,384]{3,1,0,2:T(8,128)} %copy.95), calls=%async_computation.4 | async-start | bytes 294912 | tf_op jit(solution)/shard_map/all_to_all | solution.py:180
